TPU v7x, 512 devices: a whole 4x8x8 slice. The times are simulated.
512 devices in a mesh: vocab: 64 (over z, y), hid: 4 (over x), tok: 2 (over core).
Axes of the slice: x: 4, y: 8, z: 8, core: 2. Of those that a mesh axis runs over, the one named last changes fastest.
Arguments:
- hidden: bfloat16 [1024, 8192], P('tok', ('hid', 'vocab')), may hold values from -300 to 300
- weight: bfloat16 [8192, 64128], P('hid', 'vocab'), may hold values from -0.1875 to 0.1875
- labels: int32 [1024], P('tok'), may hold values from 0 to 64127
Outputs:
- token_loss: float32 [1024], P('tok')
- mean_loss: float32 [], replicated
All inputs are finite; a program needn't handle non-finite values.
Results may differ from a plain program's by a relative error of at most 0.0003.
Values may be sent and summed in bfloat16 or wider, within the bound.
No kernel may reach another device: no remote copies, remote signals or barrier semaphores. Data moves between devices by JAX's collectives and lax.ppermute only.
A program may use at most 64 MiB of HBM per device.

v0:
```python
import functools

import jax
import jax.numpy as jnp
import numpy as np
from jax import lax
from jax.experimental import pallas as pl
from jax.experimental.pallas import tpu as pltpu
from jax.sharding import Mesh
from jax.sharding import PartitionSpec as P

SENT = jnp.float16
SENT_SCALE = 0.5
AXES = ("z", "y", "hid", "tok")


def device_ids():
    return np.arange(int(np.prod([lax.axis_size(a) for a in AXES]))).reshape(
        [lax.axis_size(a) for a in AXES]
    )


def even_groups():
    ids = device_ids()
    groups = [
        ids[z::2, y::2, x, core].reshape(-1).tolist()
        for x in range(ids.shape[2])
        for core in range(ids.shape[3])
        for z in range(2)
        for y in range(2)
    ]
    return groups


def near_groups():
    ids = device_ids()
    length, width = ids.shape[:2]
    groups = []
    for x in range(ids.shape[2]):
        for core in range(ids.shape[3]):
            for z in range(0, length, 2):
                for y in range(0, width, 2):
                    zs = sorted(((z + core) % length, (z + core + 1) % length), key=lambda n: n % 2)
                    ys = sorted(((y + core) % width, (y + core + 1) % width), key=lambda n: n % 2)
                    groups.append([int(ids[a, b, x, core]) for a in zs for b in ys])
    return groups


def sent_to_all(array, axis, groups=None):
    size = lax.axis_size(axis) if groups is None else len(groups[0])
    copies = jnp.broadcast_to(array, (size, *array.shape))
    return lax.all_to_all(
        copies, axis, split_axis=0, concat_axis=0, axis_index_groups=groups, tiled=True
    )


def gathered_features(features):
    return sent_to_all(sent_to_all(features, AXES, even_groups()), AXES, near_groups())


def matmul_kernel(found, weight_ref, out_ref, rows, *, shares, block):
    width = weight_ref.shape[0]
    side = lax.axis_size("y") // 2
    starts = range(0, width, block)
    for parity in range(found.shape[0]):
        z, y = divmod(parity, 2)
        for j in range(found.shape[1]):
            rows[(2 * (j // side) + z) * 2 * side + 2 * (j % side) + y] = found[parity, j]
    features = rows[...].reshape(-1, rows.shape[-1])
    for at in starts:
        tall = min(block, width - at)
        product = jnp.dot(weight_ref[at : at + tall], features, preferred_element_type=jnp.float32)
        across = product.shape[1] // shares
        for k in range(shares):
            out_ref[k, at : at + tall] = product[:, k * across : (k + 1) * across]


def partial_logits(found, weight, shares):
    width, depth = weight.shape
    own, tokens = found.shape[-2:]
    block = 256
    return pl.pallas_call(
        functools.partial(matmul_kernel, shares=shares, block=block),
        in_specs=[pl.BlockSpec(memory_space=pltpu.VMEM), pl.BlockSpec(memory_space=pltpu.VMEM)],
        out_specs=pl.BlockSpec(memory_space=pltpu.VMEM),
        scratch_shapes=[
            pltpu.VMEM((depth // own, own, tokens), weight.dtype),
        ],
        out_shape=jax.ShapeDtypeStruct((shares, width, tokens // shares), jnp.float32),
        compiler_params=pltpu.CompilerParams(vmem_limit_bytes=40 * 2**20),
        name="partial_logits",
    )(found, weight)


def combined(top, summed, target, axis):
    row_top = jnp.max(top, axis=axis)
    scaled = summed * jnp.exp(top - jnp.expand_dims(row_top, axis))
    return row_top, jnp.sum(scaled, axis=axis), jnp.sum(target, axis=axis)


def body(hidden, weight, labels):
    tokens = hidden.shape[0]
    hid = lax.axis_size("hid")
    share = tokens // hid
    width = weight.shape[1]
    found = gathered_features(hidden.T)
    found = found.reshape(found.shape[0], -1, *found.shape[-2:])
    blocks = partial_logits(found, weight.T, hid)
    blocks = lax.all_to_all((blocks * SENT_SCALE).astype(SENT), "hid", 0, 0, tiled=True)
    logits = jnp.sum(blocks.astype(jnp.float32), axis=0) / SENT_SCALE

    label = lax.dynamic_slice_in_dim(labels, lax.axis_index("hid") * share, share, 0)
    column = label - lax.axis_index(("z", "y")) * width
    hit = lax.broadcasted_iota(jnp.int32, logits.shape, 0) == column[None, :]
    target = jnp.sum(jnp.where(hit, logits, 0.0), axis=0)
    top = jnp.max(logits, axis=0)
    summed = jnp.sum(jnp.exp(logits - top[None, :]), axis=0)

    sent = sent_to_all(jnp.stack([top, summed, target]), ("z", "hid"))
    sent = sent.reshape(lax.axis_size("z"), hid, 3, share)
    found = combined(sent[:, :, 0], sent[:, :, 1], sent[:, :, 2], 0)
    sent = sent_to_all(jnp.stack(found).reshape(3, tokens), ("y", "tok"))
    sent = sent.reshape(lax.axis_size("y"), -1, 3, tokens)
    top, summed, target = combined(sent[:, :, 0], sent[:, :, 1], sent[:, :, 2], 0)
    losses = top + jnp.log(summed) - target
    own = lax.dynamic_index_in_dim(losses, lax.axis_index("tok"), 0, keepdims=False)
    return own, jnp.sum(losses) / losses.size


def solution(mesh):
    finer = Mesh(
        mesh.devices.reshape(8, 8, mesh.shape["hid"], mesh.shape["tok"]),
        AXES,
    )
    in_specs = (P("tok", ("hid", "z", "y")), P("hid", ("z", "y")), P("tok"))
    out_specs = (P("tok"), P())
    return jax.shard_map(body, mesh=finer, in_specs=in_specs, out_specs=out_specs, check_vma=False)
```

profile of v0, /device:TPU:1, one launch (start us, length us, event | category | flops | bytes accessed | tf_op | source)
XLA Modules:
  0.0 112.2 jit_solution(14997411414954278408)
XLA Ops:
  0.6 0.8 broadcast_in_dim.20
  1.4 34.5 %all_to_all.25 = bf16[16,32,512]{2,1,0:T(8,128)(2,1)S(1)} all-to-all(bf16[16,32,512]{2,1,0:T(8,128)(2,1)S(1)} %broadcast_in_dim.20), channel_id=1, replica_groups={{0,16,32,48,128,144,160,176,256,272,288,304,384,400,416,432},{8,24,40,5..., dimensions={0} | all-to-all | bytes 1048576 | tf_op jit(solution)/shard_map/all_to_all | solution.py:52
  35.9 0.2 broadcast_in_dim.21
  36.2 0.0 copy-start
  36.2 20.2 %all_to_all.26.found = bf16[4,16,32,512]{3,2,1,0:T(8,128)(2,1)S(1)} all-to-all(bf16[4,16,32,512]{3,2,1,0:T(8,128)(2,1)S(1)} %broadcast_in_dim.21), channel_id=1, replica_groups={{0,8,64,72},{16,24,80,88},{32,40,96,104},{48,56,112,120},{128,136,192,2..., dimensions={0} | all-to-all | bytes 4194304 | tf_op jit(solution)/shard_map/all_to_all | solution.py:52
  56.4 0.0 copy-done
  56.4 2.3 %partial_logits.1 = f32[4,1002,128]{2,1,0:T(8,128)S(1)} custom-call(bf16[4,16,32,512]{3,2,1,0:T(8,128)(2,1)S(1)} %all_to_all.26.found, bf16[1002,2048]{1,0:T(8,128)(2,1)S(1)} %bitcast.37), custom_call_target="tpu_custom_call" | custom-call | tf_op jit(solution)/shard_map/partial_logits/pallas_call | solution.py:82
  58.7 1.2 %multiply_convert_fusion = f16[4,1002,128]{2,1,0:T(8,128)(2,1)} fusion(f32[4,1002,128]{2,1,0:T(8,128)S(1)} %partial_logits.1), kind=kLoop, calls=%fused_computation.1 | loop fusion | flops 1026048 | bytes 3078144 | tf_op jit(solution)/shard_map/convert_element_type | solution.py:109
  59.8 4.0 %all-to-all-start.2 = ((f16[4,1002,128]{2,1,0:T(8,128)(2,1)}), f16[4,1002,128]{2,1,0:T(8,128)(2,1)S(1)}, u32[]{:S(2)}, u32[]{:S(2)}) async-start(f16[4,1002,128]{2,1,0:T(8,128)(2,1)} %multiply_convert_fusion), calls=%async_computation.2 | async-start | bytes 2064384 | tf_op jit(solution)/shard_map/all_to_all | solution.py:109
  63.9 0.8 dynamic-slice_subtract_fusion
  64.6 13.1 %all-to-all-done.2 = f16[4,1002,128]{2,1,0:T(8,128)(2,1)S(1)} async-done(((f16[4,1002,128]{2,1,0:T(8,128)(2,1)}), f16[4,1002,128]{2,1,0:T(8,128)(2,1)S(1)}, u32[]{:S(2)}, u32[]{:S(2)}) %all-to-all-start.2) | async-done | bytes 1026080 | tf_op jit(solution)/shard_map/all_to_all | solution.py:109
  77.7 0.1 convert_reduce_fusion
  77.8 0.1 multiply_reduce_fusion
  78.0 0.2 exponential_reduce_fusion
  78.2 15.1 %all_to_all.27 = f32[32,3,128]{2,1,0:T(4,128)S(1)} all-to-all(f32[32,3,128]{2,1,0:T(4,128)S(1)} %broadcast_in_dim.23), channel_id=1, replica_groups=mesh['z'=8,'y'=8,'hid'=4,'tok'=2] {'z','hid'}, dimensions={0} | all-to-all | bytes 98304 | tf_op jit(solution)/shard_map/all_to_all | solution.py:52
  93.4 0.7 broadcast_in_dim.24
  94.0 6.2 %all-to-all-start.4 = ((f32[16,3,512]{2,1,0:T(4,128)}), f32[16,3,512]{2,1,0:T(4,128)S(1)}, u32[]{:S(2)}, u32[]{:S(2)}) async-start(f32[16,3,512]{2,1,0:T(4,128)} %broadcast_in_dim.24), calls=%async_computation.4 | async-start | bytes 262144 | tf_op jit(solution)/shard_map/all_to_all | solution.py:52
  100.2 8.9 %all-to-all-done.4 = f32[16,3,512]{2,1,0:T(4,128)S(1)} async-done(((f32[16,3,512]{2,1,0:T(4,128)}), f32[16,3,512]{2,1,0:T(4,128)S(1)}, u32[]{:S(2)}, u32[]{:S(2)}) %all-to-all-start.4) | async-done | bytes 98336 | tf_op jit(solution)/shard_map/all_to_all | solution.py:52
  109.1 0.1 fusion.8
  109.2 0.1 fusion.1
  109.2 0.6 fusion.7
  109.8 0.6 constant_dynamic-slice_fusion
  (6 shorter events, 0.1 us)
Async XLA Ops:
  36.2 20.2 %copy-start = (bf16[2048,1002]{0,1:T(8,128)(2,1)S(1)}, bf16[2048,1002]{0,1:T(8,128)(2,1)}, u32[]{:S(2)}) copy-start(bf16[2048,1002]{0,1:T(8,128)(2,1)} %param.4) | copy-start | bytes 12312580
  59.8 17.9 %all-to-all-start.2 = ((f16[4,1002,128]{2,1,0:T(8,128)(2,1)}), f16[4,1002,128]{2,1,0:T(8,128)(2,1)S(1)}, u32[]{:S(2)}, u32[]{:S(2)}) async-start(f16[4,1002,128]{2,1,0:T(8,128)(2,1)} %multiply_convert_fusion), calls=%async_computation.2 | async-start | bytes 2064384 | tf_op jit(solution)/shard_map/all_to_all | solution.py:109
  94.0 15.1 %all-to-all-start.4 = ((f32[16,3,512]{2,1,0:T(4,128)}), f32[16,3,512]{2,1,0:T(4,128)S(1)}, u32[]{:S(2)}, u32[]{:S(2)}) async-start(f32[16,3,512]{2,1,0:T(4,128)} %broadcast_in_dim.24), calls=%async_computation.4 | async-start | bytes 262144 | tf_op jit(solution)/shard_map/all_to_all | solution.py:52
where the time goes:
time: 113 us; the launch traced here: 112 us
  blocking collectives  69.7 us (62%)
  waiting for transfers between devices  22 us (19%)
  starting transfers between devices  10.2 us (9%)
  other arithmetic  3.25 us (3%)
  between operations  2.46 us (2%)
  local copies, waits for them, and re-layouts  2.31 us (2%)
  Pallas kernels  2.28 us (2%)
    all_to_all x3, blocking collectives, sent_to_all(): lax.all_to_all(copies, axis, split_axis=0, concat_axis=0, axis_index_grou...  69.7 us
    all_to_all x1, waiting for transfers between devices, body(): lax.all_to_all((blocks * SENT_SCALE).astype(SENT), 'hid', 0, 0, tiled=True)  13.1 us
    all_to_all x1, waiting for transfers between devices, sent_to_all(): lax.all_to_all(copies, axis, split_axis=0, concat_axis=0, axis_index_grou...  8.89 us
    all_to_all x1, starting transfers between devices, sent_to_all(): lax.all_to_all(copies, axis, split_axis=0, concat_axis=0, axis_index_grou...  6.17 us
    all_to_all x1, starting transfers between devices, body(): lax.all_to_all((blocks * SENT_SCALE).astype(SENT), 'hid', 0, 0, tiled=True)  4.01 us
    pallas_call x1, Pallas kernels, partial_logits(): pl.pallas_call(functools.partial(matmul_kernel, shares=shares, block=bloc...  2.28 us
  transfers between devices with their start and end apart: 2, of which 2 were waited for; matrix products, arithmetic and copies ran while one was open for 1% of the time, Pallas kernels for 0%

commit v1 on v0

v1 whole, which is shorter than its diff:
```python
import functools

import jax
import jax.numpy as jnp
import numpy as np
from jax import lax
from jax.experimental import pallas as pl
from jax.experimental.pallas import tpu as pltpu
from jax.sharding import Mesh
from jax.sharding import PartitionSpec as P

SENT = jnp.float16
SENT_SCALE = 0.5
AXES = ("z", "y", "hid", "tok")


def device_ids():
    return np.arange(int(np.prod([lax.axis_size(a) for a in AXES]))).reshape(
        [lax.axis_size(a) for a in AXES]
    )


def lines(first):
    ids = device_ids()
    along_z, along_y = (1, 2, 0), (0, 2, 1)
    orders = (along_z, along_y) if first else (along_y, along_z)
    parts = [ids[:, :, :, core].transpose(order) for core, order in enumerate(orders)]
    return [line for part in parts for line in part[..., line_order()].reshape(-1, part.shape[-1]).tolist()]


def line_order():
    size = lax.axis_size("z")
    return [k // 2 if k % 2 == 0 else size - 1 - k // 2 for k in range(size)]


def sent_to_all(array, axis, groups=None):
    size = lax.axis_size(axis) if groups is None else len(groups[0])
    copies = jnp.broadcast_to(array, (size, *array.shape))
    return lax.all_to_all(
        copies, axis, split_axis=0, concat_axis=0, axis_index_groups=groups, tiled=True
    )


def gathered_features(features):
    return sent_to_all(sent_to_all(features, AXES, lines(True)), AXES, lines(False))


def matmul_kernel(found, weight_ref, labels, out_ref, column, core, rows, *, shares, block):
    shard = lax.axis_index("z") * lax.axis_size("y") + lax.axis_index("y")
    column[...] = labels[pl.ds(lax.axis_index("hid"), 1)] - shard * weight_ref.shape[0]
    core[...] = jnp.full(core.shape, lax.axis_index("tok"), jnp.int32)
    width = weight_ref.shape[0]
    side = lax.axis_size("y")
    starts = range(0, width, block)
    first = lax.axis_index("tok") == 0
    for i, far in enumerate(line_order()):
        for j, near in enumerate(line_order()):
            at = jnp.where(first, near * side + far, far * side + near)
            rows[at] = found[i, j]
    features = rows[...].reshape(-1, rows.shape[-1])
    for at in starts:
        tall = min(block, width - at)
        product = jnp.dot(weight_ref[at : at + tall], features, preferred_element_type=jnp.float32)
        across = product.shape[1] // shares
        for k in range(shares):
            out_ref[k, at : at + tall] = product[:, k * across : (k + 1) * across]


def partial_logits(found, weight, labels, shares):
    width, depth = weight.shape
    own, tokens = found.shape[-2:]
    block = 256
    return pl.pallas_call(
        functools.partial(matmul_kernel, shares=shares, block=block),
        in_specs=[pl.BlockSpec(memory_space=pltpu.VMEM)] * 3,
        out_specs=[pl.BlockSpec(memory_space=pltpu.VMEM)] * 3,
        scratch_shapes=[
            pltpu.VMEM((depth // own, own, tokens), weight.dtype),
        ],
        out_shape=[
            jax.ShapeDtypeStruct((shares, width, tokens // shares), jnp.float32),
            jax.ShapeDtypeStruct((1, tokens // shares), jnp.int32),
            jax.ShapeDtypeStruct((1, tokens), jnp.int32),
        ],
        compiler_params=pltpu.CompilerParams(vmem_limit_bytes=40 * 2**20),
        name="partial_logits",
    )(found, weight, labels.reshape(shares, -1))


def log_of_sum(parts, axis):
    top = jnp.max(parts, axis=axis, keepdims=True)
    return jnp.squeeze(top, axis) + jnp.log(jnp.sum(jnp.exp(parts - top), axis=axis))


def combined(parts, axis):
    sums, targets = parts
    return jnp.stack([log_of_sum(sums, axis), jnp.sum(targets, axis=axis)])


def body(hidden, weight, labels):
    tokens = hidden.shape[0]
    hid = lax.axis_size("hid")
    share = tokens // hid
    cores = lax.axis_size("tok")
    found = gathered_features(hidden.T)
    blocks, column, core = partial_logits(found, weight.T, labels, hid)
    blocks = lax.all_to_all((blocks * SENT_SCALE).astype(SENT), "hid", 0, 0, tiled=True)
    logits = jnp.sum(blocks.astype(jnp.float32), axis=0) / SENT_SCALE

    hit = lax.broadcasted_iota(jnp.int32, logits.shape, 0) == column
    target = jnp.sum(jnp.where(hit, logits, 0.0), axis=0)
    sent = sent_to_all(jnp.stack([log_of_sum(logits, 0), target]), ("z", "hid"))
    sent = sent.reshape(-1, hid, 2, share)
    found = combined((sent[:, :, 0], sent[:, :, 1]), 0).reshape(2, tokens)
    sent = sent_to_all(found, ("tok", "y")).reshape(cores, -1, 2, tokens)
    lse, target = combined((sent[:, :, 0], sent[:, :, 1]), 1)
    losses = lse - target
    own = jnp.where(core[0] == 0, losses[0], losses[1])
    return own, jnp.sum(losses) / losses.size


def solution(mesh):
    finer = Mesh(
        mesh.devices.reshape(8, 8, mesh.shape["hid"], mesh.shape["tok"]),
        AXES,
    )
    in_specs = (P("tok", ("hid", "z", "y")), P("hid", ("z", "y")), P("tok"))
    out_specs = (P("tok"), P())
    return jax.shard_map(body, mesh=finer, in_specs=in_specs, out_specs=out_specs, check_vma=False)
```

time: 113 us -> 106 us (0.938)
  blocking collectives: 69.7 us -> 97.4 us
  waiting for transfers between devices: 22 us -> 0 us
  starting transfers between devices: 10.2 us -> 0 us
  other arithmetic: 3.25 us -> 2.01 us
  local copies, waits for them, and re-layouts: 2.31 us -> 1.08 us
    all_to_all x2 -> x0, waiting for transfers between devices: 22 us -> none  [the longest x1 13.1 us: body(): lax.all_to_all((blocks * SENT_SCALE).astype(SENT), 'hid', 0, 0, tiled=True)]
    all_to_all x0 -> x1, blocking collectives: none -> 14.3 us  [body(): lax.all_to_all((blocks * SENT_SCALE).astype(SENT), 'hid', 0, 0, tiled=True)]
    all_to_all x3 -> x4, blocking collectives: 69.7 us -> 83.1 us  [sent_to_all(): lax.all_to_all(copies, axis, split_axis=0, concat_axis=0, axis_index_grou...]
    all_to_all x2 -> x0, starting transfers between devices: 10.2 us -> none  [the longest x1 6.17 us: sent_to_all(): lax.all_to_all(copies, axis, split_axis=0, concat_axis=0, axis_index_grou...]
  transfers between devices with their start and end apart: 2 -> 0, of which waited for: 2 -> 0; matrix products, arithmetic and copies ran while one was open for 1% -> 0% of each run, Pallas kernels for 0% -> 0%
where the time goes in v1:
time: 106 us; the launch traced here: 105 us
  blocking collectives  97.4 us (92%)
  between operations  2.5 us (2%)
  Pallas kernels  2.36 us (2%)
  other arithmetic  2.01 us (2%)
  local copies, waits for them, and re-layouts  1.08 us (1%)
    all_to_all x4, blocking collectives, sent_to_all(): lax.all_to_all(copies, axis, split_axis=0, concat_axis=0, axis_index_grou...  83.1 us
    all_to_all x1, blocking collectives, body(): lax.all_to_all((blocks * SENT_SCALE).astype(SENT), 'hid', 0, 0, tiled=True)  14.3 us
    pallas_call x1, Pallas kernels, partial_logits(): pl.pallas_call(functools.partial(matmul_kernel, shares=shares, block=bloc...  2.36 us

profile of v1, /device:TPU:1, one launch (start us, length us, event | category | flops | bytes accessed | tf_op | source)
XLA Modules:
  0.0 105.3 jit_solution(14177251690919462434)
XLA Ops:
  0.6 0.8 broadcast_in_dim.19
  1.4 16.1 %all_to_all.25 = bf16[8,32,512]{2,1,0:T(8,128)(2,1)S(1)} all-to-all(bf16[8,32,512]{2,1,0:T(8,128)(2,1)S(1)} %broadcast_in_dim.19), channel_id=1, replica_groups={{0,448,64,384,128,320,192,256},{2,450,66,386,130,322,194,258},{4,452,68..., dimensions={0} | all-to-all | bytes 524288 | tf_op jit(solution)/shard_map/all_to_all | solution.py:39
  17.5 0.2 broadcast_in_dim.20
  17.7 0.0 copy-start
  17.7 0.0 copy-start.1
  17.8 38.7 %all_to_all.26.found = bf16[8,8,32,512]{3,2,1,0:T(8,128)(2,1)S(1)} all-to-all(bf16[8,8,32,512]{3,2,1,0:T(8,128)(2,1)S(1)} %broadcast_in_dim.20), channel_id=1, replica_groups={{0,56,8,48,16,40,24,32},{2,58,10,50,18,42,26,34},{4,60,12,52,20,44,28,3..., dimensions={0} | all-to-all | bytes 4194304 | tf_op jit(solution)/shard_map/all_to_all | solution.py:39
  56.4 0.0 copy-done
  56.4 0.0 copy-done.1
  56.4 2.4 %partial_logits.1 = (f32[4,1002,128]{2,1,0:T(8,128)S(1)}, s32[1,128]{1,0:T(1,128)S(1)}, s32[1,512]{1,0:T(1,128)S(1)}) custom-call(bf16[8,8,32,512]{3,2,1,0:T(8,128)(2,1)S(1)} %all_to_all.26.found, bf16[1002,2048]{1,0:T(8,128)(2,1)S(1)} %bitcast.32, s32[4,128]{1,0:T(4,128)S(1)} %bitcast.33), custom_call_target="tpu_custom_call" | custom-call | tf_op jit(solution)/shard_map/partial_logits/pallas_call | solution.py:73
  58.8 0.2 multiply_convert_fusion
  59.0 14.3 %all_to_all.27 = f16[4,1002,128]{2,1,0:T(8,128)(2,1)S(1)} all-to-all(f16[4,1002,128]{2,1,0:T(8,128)(2,1)S(1)} %multiply_convert_fusion), channel_id=1, replica_groups=mesh['z'=8,'y'=8,'hid'=4,'tok'=2] {'hid'}, dimensions={0} | all-to-all | bytes 2052096 | tf_op jit(solution)/shard_map/all_to_all | solution.py:107
  73.3 0.1 convert_reduce_fusion
  73.5 0.1 multiply_reduce_fusion
  73.6 0.2 exponential_reduce_fusion
  73.9 12.5 %all_to_all.28 = f32[32,2,128]{2,1,0:T(2,128)S(1)} all-to-all(f32[32,2,128]{2,1,0:T(2,128)S(1)} %broadcast_in_dim.22), channel_id=1, replica_groups=mesh['z'=8,'y'=8,'hid'=4,'tok'=2] {'z','hid'}, dimensions={0} | all-to-all | bytes 65536 | tf_op jit(solution)/shard_map/all_to_all | solution.py:39
  86.5 15.8 %all_to_all.29 = f32[16,2,512]{2,1,0:T(2,128)S(1)} all-to-all(f32[16,2,512]{2,1,0:T(2,128)S(1)} %broadcast_in_dim.23), channel_id=1, replica_groups=mesh['z'=8,'y'=8,'hid'=4,'tok'=2] {'tok','y'}, dimensions={0} | all-to-all | bytes 131072 | tf_op jit(solution)/shard_map/all_to_all | solution.py:39
  102.4 0.6 fusion.5
  103.6 0.6 compare_select_fusion
  (12 shorter events, 0.2 us)
Async XLA Ops:
  17.7 38.7 %copy-start = (bf16[2048,1002]{0,1:T(8,128)(2,1)S(1)}, bf16[2048,1002]{0,1:T(8,128)(2,1)}, u32[]{:S(2)}) copy-start(bf16[2048,1002]{0,1:T(8,128)(2,1)} %param.4) | copy-start | bytes 12312580
  17.7 38.7 %copy-start.1 = (s32[512]{0:T(512)S(1)}, s32[512]{0:T(512)}, u32[]{:S(2)}) copy-start(s32[512]{0:T(512)} %param.5) | copy-start | bytes 6148

commit v2 on v1

--- a/solution.py
+++ b/solution.py
@@ -9,8 +9,6 @@
 from jax.sharding import Mesh
 from jax.sharding import PartitionSpec as P
 
-SENT = jnp.float16
-SENT_SCALE = 0.5
 AXES = ("z", "y", "hid", "tok")
 
 
@@ -104,8 +102,8 @@
     cores = lax.axis_size("tok")
     found = gathered_features(hidden.T)
     blocks, column, core = partial_logits(found, weight.T, labels, hid)
-    blocks = lax.all_to_all((blocks * SENT_SCALE).astype(SENT), "hid", 0, 0, tiled=True)
-    logits = jnp.sum(blocks.astype(jnp.float32), axis=0) / SENT_SCALE
+    blocks = lax.all_to_all(blocks, "hid", 0, 0, tiled=True)
+    logits = jnp.sum(blocks, axis=0)
 
     hit = lax.broadcasted_iota(jnp.int32, logits.shape, 0) == column
     target = jnp.sum(jnp.where(hit, logits, 0.0), axis=0)
@@ -116,7 +114,7 @@
     lse, target = combined((sent[:, :, 0], sent[:, :, 1]), 1)
     losses = lse - target
     own = jnp.where(core[0] == 0, losses[0], losses[1])
-    return own, jnp.sum(losses) / losses.size
+    return own, jnp.sum(losses[0] + losses[1]) / losses.size
 
 
 def solution(mesh):

time: 106 us -> 117 us (1.10)
  blocking collectives: 97.4 us -> 108 us
    all_to_all x1, blocking collectives: 14.3 us -> 25.6 us  [body(): blocks = lax.all_to_all(blocks, 'hid', 0, 0, tiled=True)]
where the time goes in v2:
time: 117 us; the launch traced here: 116 us
  blocking collectives  108 us (92%)
  between operations  2.5 us (2%)
  Pallas kernels  2.36 us (2%)
  other arithmetic  1.8 us (2%)
    all_to_all x4, blocking collectives, sent_to_all(): lax.all_to_all(copies, axis, split_axis=0, concat_axis=0, axis_index_grou...  82.9 us
    all_to_all x1, blocking collectives, body(): blocks = lax.all_to_all(blocks, 'hid', 0, 0, tiled=True)  25.6 us
    pallas_call x1, Pallas kernels, partial_logits(): pl.pallas_call(functools.partial(matmul_kernel, shares=shares, block=bloc...  2.36 us

profile of v2, /device:TPU:1, one launch (start us, length us, event | category | flops | bytes accessed | tf_op | source)
XLA Modules:
  0.0 116.2 jit_solution(16839049210215394024)
XLA Ops:
  0.6 0.8 broadcast_in_dim.19
  1.4 16.1 %all_to_all.25 = bf16[8,32,512]{2,1,0:T(8,128)(2,1)S(1)} all-to-all(bf16[8,32,512]{2,1,0:T(8,128)(2,1)S(1)} %broadcast_in_dim.19), channel_id=1, replica_groups={{0,448,64,384,128,320,192,256},{2,450,66,386,130,322,194,258},{4,452,68..., dimensions={0} | all-to-all | bytes 524288 | tf_op jit(solution)/shard_map/all_to_all | solution.py:37
  17.5 0.2 broadcast_in_dim.20
  17.7 0.0 copy-start
  17.7 0.0 copy-start.1
  17.8 38.7 %all_to_all.26.found = bf16[8,8,32,512]{3,2,1,0:T(8,128)(2,1)S(1)} all-to-all(bf16[8,8,32,512]{3,2,1,0:T(8,128)(2,1)S(1)} %broadcast_in_dim.20), channel_id=1, replica_groups={{0,56,8,48,16,40,24,32},{2,58,10,50,18,42,26,34},{4,60,12,52,20,44,28,3..., dimensions={0} | all-to-all | bytes 4194304 | tf_op jit(solution)/shard_map/all_to_all | solution.py:37
  56.4 0.0 copy-done
  56.4 0.0 copy-done.1
  56.4 2.4 %partial_logits.1 = (f32[4,1002,128]{2,1,0:T(8,128)S(1)}, s32[1,128]{1,0:T(1,128)S(1)}, s32[1,512]{1,0:T(1,128)S(1)}) custom-call(bf16[8,8,32,512]{3,2,1,0:T(8,128)(2,1)S(1)} %all_to_all.26.found, bf16[1002,2048]{1,0:T(8,128)(2,1)S(1)} %bitcast.32, s32[4,128]{1,0:T(4,128)S(1)} %bitcast.33), custom_call_target="tpu_custom_call" | custom-call | tf_op jit(solution)/shard_map/partial_logits/pallas_call | solution.py:71
  58.8 25.6 %all_to_all.27 = f32[4,1002,128]{2,1,0:T(8,128)S(1)} all-to-all(f32[4,1002,128]{2,1,0:T(8,128)S(1)} %get-tuple-element.6), channel_id=1, replica_groups=mesh['z'=8,'y'=8,'hid'=4,'tok'=2] {'hid'}, dimensions={0} | all-to-all | bytes 4104192 | tf_op jit(solution)/shard_map/all_to_all | solution.py:105
  84.4 0.2 reduce_sum.72
  84.5 0.1 reduce_max.27
  84.7 0.2 exponential_reduce_fusion
  84.9 12.3 %all_to_all.28 = f32[32,2,128]{2,1,0:T(2,128)S(1)} all-to-all(f32[32,2,128]{2,1,0:T(2,128)S(1)} %broadcast_in_dim.22), channel_id=1, replica_groups=mesh['z'=8,'y'=8,'hid'=4,'tok'=2] {'z','hid'}, dimensions={0} | all-to-all | bytes 65536 | tf_op jit(solution)/shard_map/all_to_all | solution.py:37
  97.3 15.8 %all_to_all.29 = f32[16,2,512]{2,1,0:T(2,128)S(1)} all-to-all(f32[16,2,512]{2,1,0:T(2,128)S(1)} %broadcast_in_dim.23), channel_id=1, replica_groups=mesh['z'=8,'y'=8,'hid'=4,'tok'=2] {'tok','y'}, dimensions={0} | all-to-all | bytes 131072 | tf_op jit(solution)/shard_map/all_to_all | solution.py:37
  113.2 1.2 %add_reduce_fusion = (f32[]{:T(128)}, f32[1,512]{1,0:T(1,128)}) fusion(f32[2,512]{1,0:T(2,128)S(1)} %add_subtract_fusion, s32[1,512]{1,0:T(1,128)S(1)} %get-tuple-element.5), kind=kLoop, calls=%fused_computation.18 | loop fusion | flops 2047 | bytes 8196 | tf_op jit(solution)/shard_map/reduce_sum | solution.py:117
  (13 shorter events, 0.2 us)
Async XLA Ops:
  17.7 38.7 %copy-start = (bf16[2048,1002]{0,1:T(8,128)(2,1)S(1)}, bf16[2048,1002]{0,1:T(8,128)(2,1)}, u32[]{:S(2)}) copy-start(bf16[2048,1002]{0,1:T(8,128)(2,1)} %param.4) | copy-start | bytes 12312580
  17.7 38.7 %copy-start.1 = (s32[512]{0:T(512)S(1)}, s32[512]{0:T(512)}, u32[]{:S(2)}) copy-start(s32[512]{0:T(512)} %param.5) | copy-start | bytes 6148

commit v3 on v2

--- a/solution.py
+++ b/solution.py
@@ -9,6 +9,8 @@
 from jax.sharding import Mesh
 from jax.sharding import PartitionSpec as P
 
+SENT = jnp.float16
+SENT_SCALE = 0.25
 AXES = ("z", "y", "hid", "tok")
 
 
@@ -56,12 +58,19 @@
             at = jnp.where(first, near * side + far, far * side + near)
             rows[at] = found[i, j]
     features = rows[...].reshape(-1, rows.shape[-1])
+    sums = [0.0] * shares
     for at in starts:
         tall = min(block, width - at)
         product = jnp.dot(weight_ref[at : at + tall], features, preferred_element_type=jnp.float32)
         across = product.shape[1] // shares
         for k in range(shares):
-            out_ref[k, at : at + tall] = product[:, k * across : (k + 1) * across]
+            part = product[:, k * across : (k + 1) * across]
+            out_ref[k, at : at + tall] = part
+            sums[k] += jnp.sum(part, axis=0, keepdims=True)
+    for k in range(shares):
+        centre = (sums[k] / width).astype(weight_ref.dtype).astype(jnp.float32)
+        out_ref[k, :width] = out_ref[k, :width] - centre
+        out_ref[k, width:] = centre
 
 
 def partial_logits(found, weight, labels, shares):
@@ -76,7 +85,7 @@
             pltpu.VMEM((depth // own, own, tokens), weight.dtype),
         ],
         out_shape=[
-            jax.ShapeDtypeStruct((shares, width, tokens // shares), jnp.float32),
+            jax.ShapeDtypeStruct((shares, width + 1, tokens // shares), jnp.float32),
             jax.ShapeDtypeStruct((1, tokens // shares), jnp.int32),
             jax.ShapeDtypeStruct((1, tokens), jnp.int32),
         ],
@@ -102,8 +111,9 @@
     cores = lax.axis_size("tok")
     found = gathered_features(hidden.T)
     blocks, column, core = partial_logits(found, weight.T, labels, hid)
-    blocks = lax.all_to_all(blocks, "hid", 0, 0, tiled=True)
-    logits = jnp.sum(blocks, axis=0)
+    blocks = lax.all_to_all((blocks * SENT_SCALE).astype(SENT), "hid", 0, 0, tiled=True)
+    blocks = blocks.astype(jnp.float32)
+    logits = jnp.sum(blocks[:, :-1] + blocks[:, -1:], axis=0) / SENT_SCALE
 
     hit = lax.broadcasted_iota(jnp.int32, logits.shape, 0) == column
     target = jnp.sum(jnp.where(hit, logits, 0.0), axis=0)

time: 117 us -> 106 us (0.906)
  blocking collectives: 108 us -> 97.4 us
    all_to_all x1, blocking collectives: 25.6 us -> 14.3 us  [body(): lax.all_to_all((blocks * SENT_SCALE).astype(SENT), 'hid', 0, 0, tiled=True)]
where the time goes in v3:
time: 106 us
  blocking collectives  97.4 us (92%)
  Pallas kernels  2.52 us (2%)
  between operations  2.51 us (2%)
  other arithmetic  2.15 us (2%)
  local copies, waits for them, and re-layouts  1.08 us (1%)
    all_to_all x4, blocking collectives, sent_to_all(): lax.all_to_all(copies, axis, split_axis=0, concat_axis=0, axis_index_grou...  83.1 us
    all_to_all x1, blocking collectives, body(): lax.all_to_all((blocks * SENT_SCALE).astype(SENT), 'hid', 0, 0, tiled=True)  14.3 us
    pallas_call x1, Pallas kernels, partial_logits(): pl.pallas_call(functools.partial(matmul_kernel, shares=shares, block=bloc...  2.52 us

profile of v3, /device:TPU:1, one launch (start us, length us, event | category | flops | bytes accessed | tf_op | source)
XLA Modules:
  0.0 105.7 jit_solution(14863629575556193909)
XLA Ops:
  0.6 0.8 broadcast_in_dim.19
  1.4 16.1 %all_to_all.25 = bf16[8,32,512]{2,1,0:T(8,128)(2,1)S(1)} all-to-all(bf16[8,32,512]{2,1,0:T(8,128)(2,1)S(1)} %broadcast_in_dim.19), channel_id=1, replica_groups={{0,448,64,384,128,320,192,256},{2,450,66,386,130,322,194,258},{4,452,68..., dimensions={0} | all-to-all | bytes 524288 | tf_op jit(solution)/shard_map/all_to_all | solution.py:39
  17.5 0.2 broadcast_in_dim.20
  17.7 0.0 copy-start
  17.7 0.0 copy-start.1
  17.8 38.7 %all_to_all.26.found = bf16[8,8,32,512]{3,2,1,0:T(8,128)(2,1)S(1)} all-to-all(bf16[8,8,32,512]{3,2,1,0:T(8,128)(2,1)S(1)} %broadcast_in_dim.20), channel_id=1, replica_groups={{0,56,8,48,16,40,24,32},{2,58,10,50,18,42,26,34},{4,60,12,52,20,44,28,3..., dimensions={0} | all-to-all | bytes 4194304 | tf_op jit(solution)/shard_map/all_to_all | solution.py:39
  56.4 0.0 copy-done
  56.4 0.0 copy-done.1
  56.4 2.5 %partial_logits.1 = (f32[4,1003,128]{2,1,0:T(8,128)S(1)}, s32[1,128]{1,0:T(1,128)S(1)}, s32[1,512]{1,0:T(1,128)S(1)}) custom-call(bf16[8,8,32,512]{3,2,1,0:T(8,128)(2,1)S(1)} %all_to_all.26.found, bf16[1002,2048]{1,0:T(8,128)(2,1)S(1)} %bitcast.33, s32[4,128]{1,0:T(4,128)S(1)} %bitcast.34), custom_call_target="tpu_custom_call" | custom-call | tf_op jit(solution)/shard_map/partial_logits/pallas_call | solution.py:80
  59.0 0.2 multiply_convert_fusion
  59.2 14.3 %all_to_all.27 = f16[4,1003,128]{2,1,0:T(8,128)(2,1)S(1)} all-to-all(f16[4,1003,128]{2,1,0:T(8,128)(2,1)S(1)} %multiply_convert_fusion), channel_id=1, replica_groups=mesh['z'=8,'y'=8,'hid'=4,'tok'=2] {'hid'}, dimensions={0} | all-to-all | bytes 2054144 | tf_op jit(solution)/shard_map/all_to_all | solution.py:114
  73.5 0.1 convert_element_type.7
  73.7 0.2 fusion
  73.8 0.1 multiply_reduce_fusion
  74.0 0.2 exponential_reduce_fusion
  74.2 12.5 %all_to_all.28 = f32[32,2,128]{2,1,0:T(2,128)S(1)} all-to-all(f32[32,2,128]{2,1,0:T(2,128)S(1)} %broadcast_in_dim.22), channel_id=1, replica_groups=mesh['z'=8,'y'=8,'hid'=4,'tok'=2] {'z','hid'}, dimensions={0} | all-to-all | bytes 65536 | tf_op jit(solution)/shard_map/all_to_all | solution.py:39
  86.8 15.8 %all_to_all.29 = f32[16,2,512]{2,1,0:T(2,128)S(1)} all-to-all(f32[16,2,512]{2,1,0:T(2,128)S(1)} %broadcast_in_dim.23), channel_id=1, replica_groups=mesh['z'=8,'y'=8,'hid'=4,'tok'=2] {'tok','y'}, dimensions={0} | all-to-all | bytes 131072 | tf_op jit(solution)/shard_map/all_to_all | solution.py:39
  102.7 1.2 %add_reduce_fusion = (f32[]{:T(128)}, f32[1,512]{1,0:T(1,128)}) fusion(f32[2,512]{1,0:T(2,128)S(1)} %add_subtract_fusion, s32[1,512]{1,0:T(1,128)S(1)} %get-tuple-element.5), kind=kLoop, calls=%fused_computation.22 | loop fusion | flops 2047 | bytes 8196 | tf_op jit(solution)/shard_map/reduce_sum | solution.py:127
  (14 shorter events, 0.2 us)
Async XLA Ops:
  17.7 38.7 %copy-start = (bf16[2048,1002]{0,1:T(8,128)(2,1)S(1)}, bf16[2048,1002]{0,1:T(8,128)(2,1)}, u32[]{:S(2)}) copy-start(bf16[2048,1002]{0,1:T(8,128)(2,1)} %param.4) | copy-start | bytes 12312580
  17.7 38.7 %copy-start.1 = (s32[512]{0:T(512)S(1)}, s32[512]{0:T(512)}, u32[]{:S(2)}) copy-start(s32[512]{0:T(512)} %param.5) | copy-start | bytes 6148

commit v4 on v1

--- a/solution.py
+++ b/solution.py
@@ -23,7 +23,7 @@
 def lines(first):
     ids = device_ids()
     along_z, along_y = (1, 2, 0), (0, 2, 1)
-    orders = (along_z, along_y) if first else (along_y, along_z)
+    orders = (along_y, along_z) if first else (along_z, along_y)
     parts = [ids[:, :, :, core].transpose(order) for core, order in enumerate(orders)]
     return [line for part in parts for line in part[..., line_order()].reshape(-1, part.shape[-1]).tolist()]
 
@@ -52,7 +52,7 @@
     width = weight_ref.shape[0]
     side = lax.axis_size("y")
     starts = range(0, width, block)
-    first = lax.axis_index("tok") == 0
+    first = lax.axis_index("tok") == 1
     for i, far in enumerate(line_order()):
         for j, near in enumerate(line_order()):
             at = jnp.where(first, near * side + far, far * side + near)
@@ -69,7 +69,7 @@
 def partial_logits(found, weight, labels, shares):
     width, depth = weight.shape
     own, tokens = found.shape[-2:]
-    block = 256
+    block = 512
     return pl.pallas_call(
         functools.partial(matmul_kernel, shares=shares, block=block),
         in_specs=[pl.BlockSpec(memory_space=pltpu.VMEM)] * 3,
@@ -116,7 +116,7 @@
     lse, target = combined((sent[:, :, 0], sent[:, :, 1]), 1)
     losses = lse - target
     own = jnp.where(core[0] == 0, losses[0], losses[1])
-    return own, jnp.sum(losses) / losses.size
+    return own, jnp.sum(losses[0] + losses[1]) / losses.size
 
 
 def solution(mesh):

time: 106 us -> 105 us (level)
  no operation moved by 1% of the time
where the time goes in v4:
time: 105 us
  blocking collectives  97.2 us (93%)
  between operations  2.5 us (2%)
  Pallas kernels  2.37 us (2%)
  other arithmetic  2.01 us (2%)
  local copies, waits for them, and re-layouts  1.08 us (1%)
    all_to_all x4, blocking collectives, sent_to_all(): lax.all_to_all(copies, axis, split_axis=0, concat_axis=0, axis_index_grou...  82.9 us
    all_to_all x1, blocking collectives, body(): lax.all_to_all((blocks * SENT_SCALE).astype(SENT), 'hid', 0, 0, tiled=True)  14.3 us
    pallas_call x1, Pallas kernels, partial_logits(): pl.pallas_call(functools.partial(matmul_kernel, shares=shares, block=bloc...  2.37 us

profile of v4, /device:TPU:1, one launch (start us, length us, event | category | flops | bytes accessed | tf_op | source)
XLA Modules:
  0.0 105.2 jit_solution(12403608890929592864)
XLA Ops:
  0.6 0.8 broadcast_in_dim.19
  1.4 19.3 %all_to_all.25 = bf16[8,32,512]{2,1,0:T(8,128)(2,1)S(1)} all-to-all(bf16[8,32,512]{2,1,0:T(8,128)(2,1)S(1)} %broadcast_in_dim.19), channel_id=1, replica_groups={{0,56,8,48,16,40,24,32},{2,58,10,50,18,42,26,34},{4,60,12,52,20,44,28,3..., dimensions={0} | all-to-all | bytes 524288 | tf_op jit(solution)/shard_map/all_to_all | solution.py:39
  20.7 0.2 broadcast_in_dim.20
  20.9 0.0 copy-start
  21.0 0.0 copy-start.1
  21.0 35.5 %all_to_all.26.found = bf16[8,8,32,512]{3,2,1,0:T(8,128)(2,1)S(1)} all-to-all(bf16[8,8,32,512]{3,2,1,0:T(8,128)(2,1)S(1)} %broadcast_in_dim.20), channel_id=1, replica_groups={{0,448,64,384,128,320,192,256},{2,450,66,386,130,322,194,258},{4,452,68..., dimensions={0} | all-to-all | bytes 4194304 | tf_op jit(solution)/shard_map/all_to_all | solution.py:39
  56.4 0.0 copy-done
  56.4 0.0 copy-done.1
  56.4 2.4 %partial_logits.1 = (f32[4,1002,128]{2,1,0:T(8,128)S(1)}, s32[1,128]{1,0:T(1,128)S(1)}, s32[1,512]{1,0:T(1,128)S(1)}) custom-call(bf16[8,8,32,512]{3,2,1,0:T(8,128)(2,1)S(1)} %all_to_all.26.found, bf16[1002,2048]{1,0:T(8,128)(2,1)S(1)} %bitcast.32, s32[4,128]{1,0:T(4,128)S(1)} %bitcast.33), custom_call_target="tpu_custom_call" | custom-call | tf_op jit(solution)/shard_map/partial_logits/pallas_call | solution.py:73
  58.8 0.2 multiply_convert_fusion
  59.0 14.3 %all_to_all.27 = f16[4,1002,128]{2,1,0:T(8,128)(2,1)S(1)} all-to-all(f16[4,1002,128]{2,1,0:T(8,128)(2,1)S(1)} %multiply_convert_fusion), channel_id=1, replica_groups=mesh['z'=8,'y'=8,'hid'=4,'tok'=2] {'hid'}, dimensions={0} | all-to-all | bytes 2052096 | tf_op jit(solution)/shard_map/all_to_all | solution.py:107
  73.4 0.1 convert_reduce_fusion
  73.5 0.1 multiply_reduce_fusion
  73.7 0.2 exponential_reduce_fusion
  73.9 12.3 %all_to_all.28 = f32[32,2,128]{2,1,0:T(2,128)S(1)} all-to-all(f32[32,2,128]{2,1,0:T(2,128)S(1)} %broadcast_in_dim.22), channel_id=1, replica_groups=mesh['z'=8,'y'=8,'hid'=4,'tok'=2] {'z','hid'}, dimensions={0} | all-to-all | bytes 65536 | tf_op jit(solution)/shard_map/all_to_all | solution.py:39
  86.3 15.8 %all_to_all.29 = f32[16,2,512]{2,1,0:T(2,128)S(1)} all-to-all(f32[16,2,512]{2,1,0:T(2,128)S(1)} %broadcast_in_dim.23), channel_id=1, replica_groups=mesh['z'=8,'y'=8,'hid'=4,'tok'=2] {'tok','y'}, dimensions={0} | all-to-all | bytes 131072 | tf_op jit(solution)/shard_map/all_to_all | solution.py:39
  102.2 1.2 %add_reduce_fusion = (f32[]{:T(128)}, f32[1,512]{1,0:T(1,128)}) fusion(f32[2,512]{1,0:T(2,128)S(1)} %add_subtract_fusion, s32[1,512]{1,0:T(1,128)S(1)} %get-tuple-element.5), kind=kLoop, calls=%fused_computation.21 | loop fusion | flops 2047 | bytes 8196 | tf_op jit(solution)/shard_map/reduce_sum | solution.py:119
  (13 shorter events, 0.2 us)
Async XLA Ops:
  20.9 35.5 %copy-start = (bf16[2048,1002]{0,1:T(8,128)(2,1)S(1)}, bf16[2048,1002]{0,1:T(8,128)(2,1)}, u32[]{:S(2)}) copy-start(bf16[2048,1002]{0,1:T(8,128)(2,1)} %param.4) | copy-start | bytes 12312580
  21.0 35.5 %copy-start.1 = (s32[512]{0:T(512)S(1)}, s32[512]{0:T(512)}, u32[]{:S(2)}) copy-start(s32[512]{0:T(512)} %param.5) | copy-start | bytes 6148

commit v5 on v4

--- a/solution.py
+++ b/solution.py
@@ -69,7 +69,7 @@
 def partial_logits(found, weight, labels, shares):
     width, depth = weight.shape
     own, tokens = found.shape[-2:]
-    block = 512
+    block = 256
     return pl.pallas_call(
         functools.partial(matmul_kernel, shares=shares, block=block),
         in_specs=[pl.BlockSpec(memory_space=pltpu.VMEM)] * 3,

time: 105 us -> 105 us (level)
  no operation moved by 1% of the time
where the time goes in v5:
time: 105 us
  blocking collectives  97.2 us (93%)
  between operations  2.5 us (2%)
  Pallas kernels  2.37 us (2%)
  other arithmetic  2.01 us (2%)
  local copies, waits for them, and re-layouts  1.08 us (1%)
    all_to_all x4, blocking collectives, sent_to_all(): lax.all_to_all(copies, axis, split_axis=0, concat_axis=0, axis_index_grou...  82.9 us
    all_to_all x1, blocking collectives, body(): lax.all_to_all((blocks * SENT_SCALE).astype(SENT), 'hid', 0, 0, tiled=True)  14.3 us
    pallas_call x1, Pallas kernels, partial_logits(): pl.pallas_call(functools.partial(matmul_kernel, shares=shares, block=bloc...  2.37 us

profile of v5, /device:TPU:1, one launch (start us, length us, event | category | flops | bytes accessed | tf_op | source)
XLA Modules:
  0.0 105.1 jit_solution(4098599487432943647)
XLA Ops:
  0.6 0.8 broadcast_in_dim.19
  1.4 19.3 %all_to_all.25 = bf16[8,32,512]{2,1,0:T(8,128)(2,1)S(1)} all-to-all(bf16[8,32,512]{2,1,0:T(8,128)(2,1)S(1)} %broadcast_in_dim.19), channel_id=1, replica_groups={{0,56,8,48,16,40,24,32},{2,58,10,50,18,42,26,34},{4,60,12,52,20,44,28,3..., dimensions={0} | all-to-all | bytes 524288 | tf_op jit(solution)/shard_map/all_to_all | solution.py:39
  20.7 0.2 broadcast_in_dim.20
  20.9 0.0 copy-start
  21.0 0.0 copy-start.1
  21.0 35.5 %all_to_all.26.found = bf16[8,8,32,512]{3,2,1,0:T(8,128)(2,1)S(1)} all-to-all(bf16[8,8,32,512]{3,2,1,0:T(8,128)(2,1)S(1)} %broadcast_in_dim.20), channel_id=1, replica_groups={{0,448,64,384,128,320,192,256},{2,450,66,386,130,322,194,258},{4,452,68..., dimensions={0} | all-to-all | bytes 4194304 | tf_op jit(solution)/shard_map/all_to_all | solution.py:39
  56.4 0.0 copy-done
  56.4 0.0 copy-done.1
  56.4 2.4 %partial_logits.1 = (f32[4,1002,128]{2,1,0:T(8,128)S(1)}, s32[1,128]{1,0:T(1,128)S(1)}, s32[1,512]{1,0:T(1,128)S(1)}) custom-call(bf16[8,8,32,512]{3,2,1,0:T(8,128)(2,1)S(1)} %all_to_all.26.found, bf16[1002,2048]{1,0:T(8,128)(2,1)S(1)} %bitcast.32, s32[4,128]{1,0:T(4,128)S(1)} %bitcast.33), custom_call_target="tpu_custom_call" | custom-call | tf_op jit(solution)/shard_map/partial_logits/pallas_call | solution.py:73
  58.8 0.2 multiply_convert_fusion
  59.0 14.3 %all_to_all.27 = f16[4,1002,128]{2,1,0:T(8,128)(2,1)S(1)} all-to-all(f16[4,1002,128]{2,1,0:T(8,128)(2,1)S(1)} %multiply_convert_fusion), channel_id=1, replica_groups=mesh['z'=8,'y'=8,'hid'=4,'tok'=2] {'hid'}, dimensions={0} | all-to-all | bytes 2052096 | tf_op jit(solution)/shard_map/all_to_all | solution.py:107
  73.3 0.1 convert_reduce_fusion
  73.5 0.1 multiply_reduce_fusion
  73.6 0.2 exponential_reduce_fusion
  73.9 12.3 %all_to_all.28 = f32[32,2,128]{2,1,0:T(2,128)S(1)} all-to-all(f32[32,2,128]{2,1,0:T(2,128)S(1)} %broadcast_in_dim.22), channel_id=1, replica_groups=mesh['z'=8,'y'=8,'hid'=4,'tok'=2] {'z','hid'}, dimensions={0} | all-to-all | bytes 65536 | tf_op jit(solution)/shard_map/all_to_all | solution.py:39
  86.3 15.8 %all_to_all.29 = f32[16,2,512]{2,1,0:T(2,128)S(1)} all-to-all(f32[16,2,512]{2,1,0:T(2,128)S(1)} %broadcast_in_dim.23), channel_id=1, replica_groups=mesh['z'=8,'y'=8,'hid'=4,'tok'=2] {'tok','y'}, dimensions={0} | all-to-all | bytes 131072 | tf_op jit(solution)/shard_map/all_to_all | solution.py:39
  102.2 1.2 %add_reduce_fusion = (f32[]{:T(128)}, f32[1,512]{1,0:T(1,128)}) fusion(f32[2,512]{1,0:T(2,128)S(1)} %add_subtract_fusion, s32[1,512]{1,0:T(1,128)S(1)} %get-tuple-element.5), kind=kLoop, calls=%fused_computation.21 | loop fusion | flops 2047 | bytes 8196 | tf_op jit(solution)/shard_map/reduce_sum | solution.py:119
  (13 shorter events, 0.2 us)
Async XLA Ops:
  20.9 35.5 %copy-start = (bf16[2048,1002]{0,1:T(8,128)(2,1)S(1)}, bf16[2048,1002]{0,1:T(8,128)(2,1)}, u32[]{:S(2)}) copy-start(bf16[2048,1002]{0,1:T(8,128)(2,1)} %param.4) | copy-start | bytes 12312580
  21.0 35.5 %copy-start.1 = (s32[512]{0:T(512)S(1)}, s32[512]{0:T(512)}, u32[]{:S(2)}) copy-start(s32[512]{0:T(512)} %param.5) | copy-start | bytes 6148
